TPU v7x, 32 devices: a whole 2x2x4 slice. The times are simulated.
32 devices in a mesh: dp: 8 (over z, x), seq: 4 (over y, core).
Axes of the slice: x: 2, y: 2, z: 4, core: 2. Of those that a mesh axis runs over, the one named last changes fastest.
Arguments:
- hidden: bfloat16 [8, 4096, 4096], P('dp', 'seq'), may hold values from -6 to 6
- value_weight: bfloat16 [4096, 64], replicated, may hold values from -0.09375 to 0.09375
- value_bias: float32 [64], replicated, may hold values from -1 to 1
- returns: float32 [8, 4096], P('dp', 'seq'), may hold values from -12 to 12, as said below
- task_bins: int32 [8, 4096], P('dp', 'seq'), may hold values from 0 to 63
- loss_mask: int32 [8, 4096], P('dp', 'seq'), may hold values 0 or 1
Outputs:
- targets: float32 [8, 4096], P('dp', 'seq')
- weight_grad: float32 [4096, 64], replicated
- bias_grad: float32 [64], replicated
Inputs may be any that keep to these rules, and one draw needn't show every extreme that they name: The returns of one rollout share a level and a trend along positions.
All inputs are finite; a program needn't handle non-finite values.
Results may differ from a plain program's by a relative error of at most 0.00083.
Values sent between devices are 32-bit elements.
A program may use at most 64 MiB of HBM per device.

v0:
```python
import jax
import jax.numpy as jnp
from jax import lax
from jax.sharding import PartitionSpec as P


def on_device(hidden, value_weight, value_bias, returns, task_bins, loss_mask):
    rollouts = hidden.shape[0] * lax.axis_size("dp")
    states = hidden.reshape(-1, hidden.shape[2])
    flat_returns = returns.reshape(-1)
    bins_iota = jnp.arange(value_weight.shape[1], dtype=jnp.int32)
    chosen = (task_bins.reshape(-1)[:, None] == bins_iota).astype(jnp.float32)
    valid = loss_mask.reshape(-1).astype(jnp.float32)
    onehot = chosen * valid[:, None]
    scores = jnp.dot(states, value_weight, preferred_element_type=jnp.float32)
    counts = jnp.sum(onehot, axis=0)
    summed = jnp.sum(onehot * flat_returns[:, None], axis=0)
    squares = jnp.sum(onehot * flat_returns[:, None] * flat_returns[:, None], axis=0)
    counts, summed, squares = lax.psum((counts, summed, squares), ("dp", "seq"))
    means = summed / jnp.maximum(counts, 1.0)
    second = squares - summed * means
    floor_counts = jnp.maximum(counts, 1.0)
    spread = jnp.sqrt(second / floor_counts + 0.1)
    deviation = flat_returns[:, None] - means
    targets = jnp.sum(chosen * (deviation / spread), axis=-1)
    predicted = jnp.sum((scores + value_bias) * chosen, axis=-1)
    slope = valid * jnp.clip(predicted - targets, -1.0, 1.0) / rollouts
    coefficient = chosen * slope[:, None]
    weight_grad = lax.dot_general(
        states,
        coefficient.astype(jnp.bfloat16),
        (((0,), (0,)), ((), ())),
        preferred_element_type=jnp.float32,
    )
    bias_grad = jnp.sum(coefficient, axis=0)
    weight_grad, bias_grad = lax.psum((weight_grad, bias_grad), ("dp", "seq"))
    return (targets.reshape(returns.shape), weight_grad, bias_grad)


def solution(mesh):
    placed = (P("dp", "seq", None), P(), P(), P("dp", "seq"), P("dp", "seq"), P("dp", "seq"))
    return jax.shard_map(
        on_device, mesh=mesh, in_specs=placed, out_specs=(P("dp", "seq"), P(), P()), check_vma=False
    )
```

profile of v0, /device:TPU:0, one launch (start us, length us, event | category | flops | bytes accessed | tf_op | source)
XLA Modules:
  0.0 201.0 jit_solution(13949442704553326158)
XLA Ops:
  7.2 0.0 copy-start
  7.2 0.0 copy-start.2
  7.2 0.0 all-reduce.3.cloned.1.call-start
  7.2 0.7 convert_element_type.17
  8.0 0.9 fusion.17
  8.9 42.0 %all-reduce = (f32[64]{0:T(128)S(1)}, f32[64]{0:T(128)S(1)}, f32[64]{0:T(128)S(1)}) all-reduce(f32[64]{0:T(128)S(1)} %get-tuple-element.4, f32[64]{0:T(128)S(1)} %get-tuple-element.3, f32[64]{0:T(128)S(1)} %get-tuple-element.5), channel_id=1, replica_groups=mesh['dp'=8,'seq'=4] {'dp','seq'}, use_global_device_ids=true, to_apply=%region_5.0 | all-reduce | flops 192 | bytes 1536 | tf_op jit(solution)/shard_map/psum | solution.py:19
  50.9 0.0 copy-start.1
  50.9 1.0 select_reduce_fusion.2
  51.9 0.0 copy-done
  51.9 0.0 copy-start.3
  51.9 6.3 %fusion.13 = f32[1024]{0:T(1024)S(1)} fusion(bf16[4096,64]{0,1:T(8,128)(2,1)S(1)} %copy-done, bf16[1,1024,4096]{2,1,0:T(8,128)(2,1)} %param.6, f32[64]{0:T(128)} %param.8, s32[1024]{0:T(1024)} %bitcast.22), kind=kOutput, calls=%fused_computation.7 | convolution fusion | flops 537132032 | bytes 8921344 | tf_op jit(solution)/shard_map/dot_general | solution.py:15
  58.2 0.0 copy-done.2
  58.2 0.0 copy-done.1
  58.3 2.5 %fusion.4 = f32[4096,64]{0,1:T(8,128)} fusion(bf16[1,1024,4096]{2,1,0:T(8,128)(2,1)S(1)} %copy-done.1, f32[1024]{0:T(1024)S(1)} %multiply_multiply_fusion, s32[1024]{0:T(1024)S(1)} %bitcast.23), kind=kOutput, calls=%fused_computation.4 | convolution fusion | flops 537001984 | bytes 9445376 | tf_op jit(solution)/shard_map/dot_general | solution.py:29
  60.8 0.0 copy-done.3
  60.8 0.0 all-reduce.3.cloned.1.call-update
  60.8 0.1 select_reduce_fusion
  61.0 40.3 %psum.39 = f32[64]{0:T(128)} all-reduce(f32[64]{0:T(128)S(1)} %select_reduce_fusion), channel_id=1, replica_groups=mesh['dp'=8,'seq'=4] {'dp','seq'}, use_global_device_ids=true, to_apply=%region_10.11 | all-reduce | flops 64 | bytes 512 | tf_op jit(solution)/shard_map/psum | solution.py:36
  101.3 90.6 %all-reduce.3.cloned.1.call-done = f32[4096,64]{0,1:T(8,128)} async-done(((f32[4096,64]{0,1:T(8,128)}), f32[4096,64]{0,1:T(8,128)}) %all-reduce.3.cloned.1.call-update) | async-done | bytes 1048592 | tf_op jit(solution)/shard_map/psum | solution.py:36
  191.9 2.3 %copy.10 = f32[4096,64]{0,1:T(8,128)} copy(f32[4096,64]{0,1:T(8,128)} %all-reduce.3.cloned.1.call-done) | data formatting | bytes 2097152
  (2 shorter events, 0.0 us)
Async XLA Ops:
  7.2 44.8 %copy-start = (bf16[4096,64]{0,1:T(8,128)(2,1)S(1)}, bf16[4096,64]{0,1:T(8,128)(2,1)}, u32[]{:S(2)}) copy-start(bf16[4096,64]{0,1:T(8,128)(2,1)} %param.7) | copy-start | bytes 1572868
  7.2 51.1 %copy-start.2 = (s32[1,1024]{1,0:T(1,128)S(1)}, s32[1,1024]{1,0:T(1,128)}, u32[]{:S(2)}) copy-start(s32[1,1024]{1,0:T(1,128)} %param.10) | copy-start | bytes 12292
  7.2 184.7 %all-reduce.3.cloned.1.call-start = ((), (), s32[]{:S(2)}) async-start(), calls=%async_computation | async-start | bytes 2097152 | tf_op jit(solution)/shard_map/psum | solution.py:36
  50.9 7.3 %copy-start.1 = (bf16[1,1024,4096]{2,1,0:T(8,128)(2,1)S(1)}, bf16[1,1024,4096]{2,1,0:T(8,128)(2,1)}, u32[]{:S(2)}) copy-start(bf16[1,1024,4096]{2,1,0:T(8,128)(2,1)} %param.6) | copy-start | bytes 25165828
  51.9 8.9 %copy-start.3 = (f32[1024]{0:T(1024)}, f32[1024]{0:T(1024)S(1)}, u32[]{:S(2)}) copy-start(f32[1024]{0:T(1024)S(1)} %select_reduce_fusion.2) | copy-start | bytes 12292
Sparse Core Ops, SparseCore 0:
  60.9 130.8 all-reduce.2
where the time goes:
time: 202 us; the launch traced here: 201 us
  waiting for transfers between devices  90.6 us (45%)
  blocking collectives  82.4 us (41%)
  between operations  14.1 us (7%)
  matrix products  8.82 us (4%)
  other arithmetic  2.77 us (1%)
  local copies, waits for them, and re-layouts  2.3 us (1%)
    psum x1, waiting for transfers between devices, on_device(): weight_grad, bias_grad = lax.psum((weight_grad, bias_grad), ('dp', 'seq'))  90.6 us
    psum x1, blocking collectives, on_device(): counts, summed, squares = lax.psum((counts, summed, squares), ('dp', 'seq'))  42 us
    psum x1, blocking collectives, on_device(): weight_grad, bias_grad = lax.psum((weight_grad, bias_grad), ('dp', 'seq'))  40.3 us
    dot_general x1, matrix products, on_device(): scores = jnp.dot(states, value_weight, preferred_element_type=jnp.float32)  6.27 us
  transfers between devices with their start and end apart: 1, of which 1 were waited for; matrix products, arithmetic and copies ran while one was open for 0% of the time, Pallas kernels for 0%

commit v1 on v0

v1 whole, which is shorter than its diff:
```python
import functools

import jax
import jax.numpy as jnp
from jax import lax
from jax.experimental import pallas as pl
from jax.experimental.pallas import tpu as pltpu
from jax.sharding import PartitionSpec as P

MESH = pl.DeviceIdType.MESH
LANES = 128
TOKENS = 256


def split_in_two(n):
    return 2 if n % 2 == 0 else 1


def plan(ndp, nseq, tiles):
    core, x = split_in_two(nseq), split_in_two(ndp)
    sizes = {"core": core, "y": nseq // core, "x": x, "z": ndp // x}
    streams = 4
    while streams > 1 and (tiles % (streams * ndp * nseq) or tiles % (streams * core * 8)):
        streams //= 2
    return sizes, streams


def kernel(ndp, nseq, rollouts, sizes, streams, hidden, weight, bias, returns, bins, mask,
           targets, grad, bias_grad, *scratch):
    (held, acc, whole, coef, predicted, turned, small, small_in, row_in, hid_sem,
     small_send, small_recv) = scratch[:12]
    stage_scratch = scratch[12:]
    tasks, width = weight.shape
    tokens = hidden.shape[0]
    tiles = acc.shape[0]
    dp, seq = lax.axis_index("dp"), lax.axis_index("seq")
    core, y = lax.rem(seq, sizes["core"]), lax.div(seq, sizes["core"])
    x, z = lax.rem(dp, sizes["x"]), lax.div(dp, sizes["x"])

    barrier = pltpu.get_barrier_semaphore()
    for r in range(1, nseq):
        pl.semaphore_signal(barrier, inc=1, device_id={"seq": lax.rem(seq + r, nseq)}, device_id_type=MESH)
    for r in range(1, ndp):
        pl.semaphore_signal(barrier, inc=1, device_id={"dp": lax.rem(dp + r, ndp)}, device_id_type=MESH)

    loads = []
    for j in range(tokens // TOKENS):
        rows = pl.ds(j * TOKENS, TOKENS)
        loads.append(pltpu.make_async_copy(hidden.at[rows], held.at[rows], hid_sem.at[j]))
        loads[-1].start()

    def peer(name, r):
        n = sizes[name]
        if name == "core":
            return {"seq": y * n + lax.rem(core + r, n)}
        if name == "y":
            return {"seq": lax.rem(y + r, n) * sizes["core"] + core}
        if name == "x":
            return {"dp": z * n + lax.rem(x + r, n)}
        return {"dp": lax.rem(z + r, n) * sizes["x"] + x}

    place = {"core": core, "y": y, "x": x, "z": z}

    def small_start(k, axis):
        n, me = (nseq, seq) if axis == "seq" else (ndp, dp)
        landing = small_in if axis == "seq" else row_in
        base = 0 if axis == "seq" else nseq - 1
        copies = []
        for r in range(1, n):
            copies.append(pltpu.make_async_remote_copy(
                src_ref=small.at[2 * k + (axis == "dp")], dst_ref=landing.at[k, r - 1],
                send_sem=small_send.at[k, base + r - 1], recv_sem=small_recv.at[k, base + r - 1],
                device_id={axis: lax.rem(me + r, n)}, device_id_type=MESH))
            copies[-1].start()
        return copies

    def small_finish(k, axis, copies):
        landing = small_in if axis == "seq" else row_in
        total = small[2 * k + (axis == "dp")]
        for r, copy in enumerate(copies):
            copy.wait()
            total = total + landing[k, r]
        return total

    def onehot_of(block):
        chosen = bins[:, block] == lax.broadcasted_iota(jnp.int32, (tasks, LANES), 0)
        return chosen, mask[:, block].astype(jnp.float32)

    blocks = [pl.ds(k * LANES, LANES) for k in range(tokens // LANES)]
    counted = summed = squared = jnp.zeros((tasks, LANES), jnp.float32)
    for block in blocks:
        chosen, valid = onehot_of(block)
        value = returns[:, block]
        counted = counted + jnp.where(chosen, valid, 0.0)
        summed = summed + jnp.where(chosen, valid * value, 0.0)
        squared = squared + jnp.where(chosen, valid * value * value, 0.0)
    lane = lax.broadcasted_iota(jnp.int32, (tasks, LANES), 1)
    columns = jnp.zeros((tasks, LANES), jnp.float32)
    for k, part in enumerate((counted, summed, squared)):
        columns = jnp.where(lane == k, jnp.sum(part, axis=1, keepdims=True), columns)
    turned[...] = jnp.zeros_like(turned)
    turned[0:tasks, :] = columns
    turned[tasks:tasks + 1, 0:tasks] = bias[...]
    across = turned[...].T
    bias_column = across[0:tasks, tasks:tasks + 1]
    small[0] = across[0:8, :]

    pl.semaphore_wait(barrier, nseq + ndp - 2)
    copies = small_start(0, "seq")

    def score(j):
        loads[j].wait()
        scores = lax.dot_general(
            weight[...], held[pl.ds(j * TOKENS, TOKENS), :], (((1,), (1,)), ((), ())),
            preferred_element_type=jnp.float32)
        for k in range(TOKENS // LANES):
            block = pl.ds(j * TOKENS + k * LANES, LANES)
            chosen, valid = onehot_of(block)
            predicted[:, block] = jnp.sum(
                jnp.where(chosen, scores[:, k * LANES:(k + 1) * LANES] + bias_column, 0.0),
                axis=0, keepdims=True)

    score(0)
    small[1] = small_finish(0, "seq", copies)
    copies = small_start(0, "dp")
    for j in range(1, tokens // TOKENS):
        score(j)
    turned[0:8, :] = small_finish(0, "dp", copies)

    across = turned[...].T
    counts, sums, squares = (across[0:tasks, k:k + 1] for k in range(3))
    floor_counts = jnp.maximum(counts, 1.0)
    means = sums / floor_counts
    spread = jnp.sqrt((squares - sums * means) / floor_counts + 0.1)
    means, spread = (jnp.broadcast_to(v, (tasks, LANES)) for v in (means, spread))
    gathered = jnp.zeros((tasks, LANES), jnp.float32)
    for block in blocks:
        chosen, valid = onehot_of(block)
        mean = jnp.sum(jnp.where(chosen, means, 0.0), axis=0, keepdims=True)
        scale = jnp.sum(jnp.where(chosen, spread, 0.0), axis=0, keepdims=True)
        target = (returns[:, block] - mean) / scale
        targets[:, block] = target
        slope = valid * jnp.clip(predicted[:, block] - target, -1.0, 1.0) / rollouts
        part = jnp.where(chosen, slope, 0.0)
        gathered = gathered + part
        coef[:, block] = part.astype(jnp.bfloat16)

    half = tiles // (streams * sizes["core"])

    def multiply(stream, which):
        first = stream * (tiles // streams) + which * half
        done = 0
        while done < half:
            now = min(32, half - done)
            start = pl.multiple_of((first + done) * (LANES // 8), LANES)
            product = jnp.dot(coef[...], held[:, pl.ds(start, now * (LANES // 8))],
                              preferred_element_type=jnp.float32)
            for b in range(now // 8):
                acc[pl.ds(first + done + b * 8, 8)] = product[:, b * LANES:(b + 1) * LANES].reshape(8, 8, LANES)
            done += now

    orders = [("core", "x", "y", "z"), ("core", "y", "x", "z")]

    class Stream:
        def __init__(self, index):
            self.index = index
            self.start = index * (tiles // streams)
            self.length = tiles // streams
            self.stage = 0
            self.path = []
            self.names = [n for n in orders[index % 2]]

        def scatter_start(self):
            name = self.names[self.stage]
            n, me = sizes[name], place[name]
            piece = self.length // n
            landing, send, recv = stage_scratch[3 * self.stage:3 * self.stage + 3]
            self.copies = []
            for r in range(1, n):
                self.copies.append(pltpu.make_async_remote_copy(
                    src_ref=acc.at[pl.ds(self.start + lax.rem(me + r, n) * piece, piece)],
                    dst_ref=landing.at[self.index, r - 1, pl.ds(0, piece)],
                    send_sem=send.at[0, self.index, r - 1], recv_sem=recv.at[0, self.index, r - 1],
                    device_id=peer(name, r), device_id_type=MESH))
                self.copies[-1].start()

        def scatter_finish(self, last):
            name = self.names[self.stage]
            n, me = sizes[name], place[name]
            piece = self.length // n
            landing = stage_scratch[3 * self.stage]
            self.path.append((self.start, piece))
            mine = pl.ds(self.start + me * piece, piece)
            total = acc[mine]
            for r, copy in enumerate(self.copies):
                copy.wait()
                total = total + landing[self.index, r, 0:piece]
            (whole if last else acc)[mine] = total
            self.start, self.length = self.start + me * piece, piece
            self.stage += 1

        def gather_start(self):
            self.stage -= 1
            name = self.names[self.stage]
            n, me = sizes[name], place[name]
            landing, send, recv = stage_scratch[3 * self.stage:3 * self.stage + 3]
            start, piece = self.path[self.stage]
            self.sent, self.due = [], []
            for r in range(1, n):
                for at, into in ((me, self.sent), (lax.rem(me + n - r, n), self.due)):
                    block = pl.ds(start + at * piece, piece)
                    into.append(pltpu.make_async_remote_copy(
                        src_ref=whole.at[block], dst_ref=whole.at[block],
                        send_sem=send.at[1, self.index, r - 1], recv_sem=recv.at[1, self.index, r - 1],
                        device_id=peer(name, r), device_id_type=MESH))
                self.sent[-1].start()

        def gather_finish(self):
            for sent, due in zip(self.sent, self.due):
                sent.wait_send()
                due.wait_recv()

    work = [Stream(i) for i in range(streams)]
    for stream in work:
        for r in range(1, sizes["core"]):
            multiply(stream.index, lax.rem(core + r, sizes["core"]))
        stream.scatter_start()
    for stream in work:
        multiply(stream.index, core)
        stream.scatter_finish(False)
        stream.scatter_start()

    turned[0:tasks, :] = jnp.where(lane == 0, jnp.sum(gathered, axis=1, keepdims=True), 0.0)
    small[2] = turned[...].T[0:8, :]
    copies = small_start(1, "seq")
    for stage in (1, 2):
        for stream in work:
            stream.scatter_finish(False)
            stream.scatter_start()
        if stage == 1:
            small[3] = small_finish(1, "seq", copies)
            copies = small_start(1, "dp")
    for stream in work:
        stream.scatter_finish(True)
        stream.gather_start()
    bias_grad[...] = small_finish(1, "dp", copies)[0:1, 0:tasks]
    for stage in range(3):
        for stream in work:
            stream.gather_finish()
            stream.gather_start()
    for stream in work:
        stream.gather_finish()
        first, count = stream.index * (tiles // streams) // 8, tiles // streams // 8
        for b in range(first, first + count):
            grad[:, b * LANES:(b + 1) * LANES] = whole[b * 8:(b + 1) * 8].reshape(tasks, LANES)


def solution(mesh):
    ndp, nseq = mesh.shape["dp"], mesh.shape["seq"]

    def on_device(hidden, value_weight, value_bias, returns, task_bins, loss_mask):
        width, tasks = value_weight.shape
        tokens = hidden.shape[0] * hidden.shape[1]
        rollouts = hidden.shape[0] * ndp
        tiles = width * tasks // (8 * LANES)
        sizes, streams = plan(ndp, nseq, tiles)
        f32 = jnp.float32
        stages = []
        length = tiles // streams
        for name in ("core", "y", "x", "z"):
            n = sizes[name]
            if name in ("y", "x"):
                n = max(sizes["y"], sizes["x"])
                piece = length // min(sizes["y"], sizes["x"])
                if name == "x":
                    piece = length
            else:
                piece = length // n
            stages += [
                pltpu.VMEM((streams, max(n - 1, 1), piece, 8, LANES), f32),
                pltpu.SemaphoreType.DMA((2, streams, max(n - 1, 1))),
                pltpu.SemaphoreType.DMA((2, streams, max(n - 1, 1))),
            ]
            length = length // sizes[name]
        vmem = pl.BlockSpec(memory_space=pltpu.VMEM)
        targets, grad, bias_grad = pl.pallas_call(
            functools.partial(kernel, ndp, nseq, rollouts, sizes, streams),
            out_shape=(
                jax.ShapeDtypeStruct((1, tokens), f32),
                jax.ShapeDtypeStruct((tasks, width), f32),
                jax.ShapeDtypeStruct((1, tasks), f32),
            ),
            in_specs=[pl.BlockSpec(memory_space=pl.ANY)] + [vmem] * 5,
            out_specs=(vmem, vmem, vmem),
            scratch_shapes=[
                pltpu.VMEM((tokens, width), jnp.bfloat16),
                pltpu.VMEM((tiles, 8, LANES), f32),
                pltpu.VMEM((tiles, 8, LANES), f32),
                pltpu.VMEM((tasks, tokens), jnp.bfloat16),
                pltpu.VMEM((1, tokens), f32),
                pltpu.VMEM((LANES, LANES), f32),
                pltpu.VMEM((4, 8, LANES), f32),
                pltpu.VMEM((2, max(nseq - 1, 1), 8, LANES), f32),
                pltpu.VMEM((2, max(ndp - 1, 1), 8, LANES), f32),
                pltpu.SemaphoreType.DMA((tokens // TOKENS,)),
                pltpu.SemaphoreType.DMA((2, nseq + ndp)),
                pltpu.SemaphoreType.DMA((2, nseq + ndp)),
            ] + stages,
            compiler_params=pltpu.CompilerParams(
                collective_id=0, has_side_effects=True, vmem_limit_bytes=56 * 1024 * 1024),
        )(hidden.reshape(tokens, width), value_weight.T, value_bias.reshape(1, tasks),
          returns.reshape(1, tokens), task_bins.reshape(1, tokens), loss_mask.reshape(1, tokens))
        return targets.reshape(returns.shape), grad.T, bias_grad.reshape(tasks)

    placed = (P("dp", "seq", None), P(), P(), P("dp", "seq"), P("dp", "seq"), P("dp", "seq"))
    return jax.shard_map(
        on_device, mesh=mesh, in_specs=placed, out_specs=(P("dp", "seq"), P(), P()), check_vma=False
    )
```

time: 202 us -> 46.7 us (0.23)
  waiting for transfers between devices: 90.6 us -> 0 us
  blocking collectives: 82.4 us -> 0 us
  Pallas kernels: 0 us -> 41.1 us
  between operations: 14.1 us -> 0.64 us
  matrix products: 8.82 us -> 0 us
  other arithmetic: 2.77 us -> 0 us
  local copies, waits for them, and re-layouts: 2.3 us -> 4.68 us
    psum x1 -> x0, waiting for transfers between devices: 90.6 us -> none  [on_device(): weight_grad, bias_grad = lax.psum((weight_grad, bias_grad), ('dp', 'seq'))]
    psum x2 -> x0, blocking collectives: 82.4 us -> none  [the longest x1 42 us: on_device(): counts, summed, squares = lax.psum((counts, summed, squares), ('dp', 'seq'))]
    pallas_call x0 -> x1, Pallas kernels: none -> 41.1 us  [on_device(): pl.pallas_call(functools.partial(kernel, ndp, nseq, rollouts, sizes, stre...]
    dot_general x2 -> x0, matrix products: 8.82 us -> none  [the longest x1 6.27 us: on_device(): scores = jnp.dot(states, value_weight, preferred_element_type=jnp.float32)]
    unnamed x9 -> x3, local copies, waits for them, and re-layouts: 2.3 us -> 4.68 us
  transfers between devices with their start and end apart: 1 -> 0, of which waited for: 1 -> 0; matrix products, arithmetic and copies ran while one was open for 0% -> 0% of each run, Pallas kernels for 0% -> 0%
where the time goes in v1:
time: 46.7 us; the launch traced here: 46.5 us
  Pallas kernels  41.1 us (88%)
  local copies, waits for them, and re-layouts  4.68 us (10%)
  between operations  0.64 us (1%)
    pallas_call x1, Pallas kernels, on_device(): pl.pallas_call(functools.partial(kernel, ndp, nseq, rollouts, sizes, stre...  41.1 us
    unnamed x3, local copies, waits for them, and re-layouts  4.68 us

profile of v1, /device:TPU:0, one launch (start us, length us, event | category | flops | bytes accessed | tf_op | source)
XLA Modules:
  0.0 46.5 jit_solution(4771025257315789180)
XLA Ops:
  0.6 41.1 %shard_map.85 = (f32[1,1024]{1,0:T(1,128)}, f32[64,4096]{1,0:T(8,128)}, f32[1,64]{1,0:T(1,128)}) custom-call(bf16[1024,4096]{1,0:T(8,128)(2,1)} %bitcast.5, bf16[64,4096]{1,0:T(8,128)(2,1)} %bitcast.7, f32[1,64]{1,0:T(1,128)} %bitcast.8, f32[1,1024]{1,0:T(1,128)} %returns.1, s32[1,1024]{1,0:T(1,128)} %bins.1, s32[1,1024]{1,0:T(1,128)} %mask.1), custom_call_target="tpu_custom_call" | custom-call | tf_op jit(solution)/shard_map/pallas_call | solution.py:286
  41.8 1.3 %copy.12 = f32[1,1024]{1,0:T(1,128)} copy(f32[1,1024]{1,0:T(1,128)} %get-tuple-element.12) | data formatting | bytes 8192
  43.1 2.3 %copy.13 = f32[4096,64]{0,1:T(8,128)} copy(f32[4096,64]{0,1:T(8,128)} %bitcast.6) | data formatting | bytes 2097152
  45.3 1.1 %copy.14 = f32[64]{0:T(128)} copy(f32[64]{0:T(128)} %bitcast.9) | data formatting | bytes 512

commit v2 on v1

--- a/solution.py
+++ b/solution.py
@@ -9,7 +9,8 @@
 
 MESH = pl.DeviceIdType.MESH
 LANES = 128
-TOKENS = 256
+TOKENS = 512
+AHEAD = 3
 
 
 def split_in_two(n):
@@ -25,11 +26,11 @@
     return sizes, streams
 
 
-def kernel(ndp, nseq, rollouts, sizes, streams, hidden, weight, bias, returns, bins, mask,
+def kernel(ndp, nseq, rollouts, sizes, streams, hidden, far_weight, far_bias, far_returns, far_bins, far_mask,
            targets, grad, bias_grad, *scratch):
-    (held, acc, whole, coef, predicted, turned, small, small_in, row_in, hid_sem,
-     small_send, small_recv) = scratch[:12]
-    stage_scratch = scratch[12:]
+    (weight, bias, returns, bins, mask, load_sem, held, acc, whole, coef, predicted, turned, small, small_in, row_in, hid_sem,
+     small_send, small_recv) = scratch[:18]
+    stage_scratch = scratch[18:]
     tasks, width = weight.shape
     tokens = hidden.shape[0]
     tiles = acc.shape[0]
@@ -43,6 +44,10 @@
     for r in range(1, ndp):
         pl.semaphore_signal(barrier, inc=1, device_id={"dp": lax.rem(dp + r, ndp)}, device_id_type=MESH)
 
+    early = [pltpu.make_async_copy(far, near, load_sem.at[k]) for k, (far, near) in enumerate(
+        ((far_returns, returns), (far_bins, bins), (far_mask, mask), (far_bias, bias), (far_weight, weight)))]
+    for copy in early:
+        copy.start()
     loads = []
     for j in range(tokens // TOKENS):
         rows = pl.ds(j * TOKENS, TOKENS)
@@ -86,6 +91,8 @@
         chosen = bins[:, block] == lax.broadcasted_iota(jnp.int32, (tasks, LANES), 0)
         return chosen, mask[:, block].astype(jnp.float32)
 
+    for copy in early[:4]:
+        copy.wait()
     blocks = [pl.ds(k * LANES, LANES) for k in range(tokens // LANES)]
     counted = summed = squared = jnp.zeros((tasks, LANES), jnp.float32)
     for block in blocks:
@@ -105,9 +112,6 @@
     bias_column = across[0:tasks, tasks:tasks + 1]
     small[0] = across[0:8, :]
 
-    pl.semaphore_wait(barrier, nseq + ndp - 2)
-    copies = small_start(0, "seq")
-
     def score(j):
         loads[j].wait()
         scores = lax.dot_general(
@@ -120,6 +124,9 @@
                 jnp.where(chosen, scores[:, k * LANES:(k + 1) * LANES] + bias_column, 0.0),
                 axis=0, keepdims=True)
 
+    early[4].wait()
+    pl.semaphore_wait(barrier, nseq + ndp - 2)
+    copies = small_start(0, "seq")
     score(0)
     small[1] = small_finish(0, "seq", copies)
     copies = small_start(0, "dp")
@@ -221,12 +228,18 @@
                 due.wait_recv()
 
     work = [Stream(i) for i in range(streams)]
-    for stream in work:
+    def send_off(stream):
         for r in range(1, sizes["core"]):
             multiply(stream.index, lax.rem(core + r, sizes["core"]))
         stream.scatter_start()
-    for stream in work:
+
+    ahead = min(AHEAD, streams)
+    for stream in work[:ahead]:
+        send_off(stream)
+    for i, stream in enumerate(work):
         multiply(stream.index, core)
+        if i + ahead < streams:
+            send_off(work[i + ahead])
         stream.scatter_finish(False)
         stream.scatter_start()
 
@@ -253,6 +266,18 @@
         first, count = stream.index * (tiles // streams) // 8, tiles // streams // 8
         for b in range(first, first + count):
             grad[:, b * LANES:(b + 1) * LANES] = whole[b * 8:(b + 1) * 8].reshape(tasks, LANES)
+
+
+def finish(targets, grad, bias_grad, targets_out, grad_out, bias_out, sem):
+    copies = [
+        pltpu.make_async_copy(grad, grad_out, sem.at[0]),
+        pltpu.make_async_copy(targets, targets_out, sem.at[1]),
+        pltpu.make_async_copy(bias_grad, bias_out, sem.at[2]),
+    ]
+    for copy in copies:
+        copy.start()
+    for copy in copies:
+        copy.wait()
 
 
 def solution(mesh):
@@ -286,13 +311,19 @@
         targets, grad, bias_grad = pl.pallas_call(
             functools.partial(kernel, ndp, nseq, rollouts, sizes, streams),
             out_shape=(
-                jax.ShapeDtypeStruct((1, tokens), f32),
-                jax.ShapeDtypeStruct((tasks, width), f32),
-                jax.ShapeDtypeStruct((1, tasks), f32),
+                pltpu.VMEM((1, tokens), f32),
+                pltpu.VMEM((tasks, width), f32),
+                pltpu.VMEM((1, tasks), f32),
             ),
-            in_specs=[pl.BlockSpec(memory_space=pl.ANY)] + [vmem] * 5,
+            in_specs=[pl.BlockSpec(memory_space=pl.ANY)] * 6,
             out_specs=(vmem, vmem, vmem),
             scratch_shapes=[
+                pltpu.VMEM((tasks, width), jnp.bfloat16),
+                pltpu.VMEM((1, tasks), f32),
+                pltpu.VMEM((1, tokens), f32),
+                pltpu.VMEM((1, tokens), jnp.int32),
+                pltpu.VMEM((1, tokens), jnp.int32),
+                pltpu.SemaphoreType.DMA((5,)),
                 pltpu.VMEM((tokens, width), jnp.bfloat16),
                 pltpu.VMEM((tiles, 8, LANES), f32),
                 pltpu.VMEM((tiles, 8, LANES), f32),
@@ -307,9 +338,21 @@
                 pltpu.SemaphoreType.DMA((2, nseq + ndp)),
             ] + stages,
             compiler_params=pltpu.CompilerParams(
-                collective_id=0, has_side_effects=True, vmem_limit_bytes=56 * 1024 * 1024),
+                collective_id=0, has_side_effects=True, vmem_limit_bytes=62 * 1024 * 1024 + 512 * 1024),
         )(hidden.reshape(tokens, width), value_weight.T, value_bias.reshape(1, tasks),
           returns.reshape(1, tokens), task_bins.reshape(1, tokens), loss_mask.reshape(1, tokens))
+        hbm = pl.BlockSpec(memory_space=pltpu.HBM)
+        targets, grad, bias_grad = pl.pallas_call(
+            finish,
+            out_shape=(
+                jax.ShapeDtypeStruct((1, tokens), f32),
+                jax.ShapeDtypeStruct((tasks, width), f32),
+                jax.ShapeDtypeStruct((1, tasks), f32),
+            ),
+            in_specs=[vmem] * 3,
+            out_specs=(hbm, hbm, hbm),
+            scratch_shapes=[pltpu.SemaphoreType.DMA((3,))],
+        )(*(pltpu.with_memory_space_constraint(v, pltpu.VMEM) for v in (targets, grad, bias_grad)))
         return targets.reshape(returns.shape), grad.T, bias_grad.reshape(tasks)
 
     placed = (P("dp", "seq", None), P(), P(), P("dp", "seq"), P("dp", "seq"), P("dp", "seq"))

time: 46.7 us -> 41.5 us (0.89)
  local copies, waits for them, and re-layouts: 4.68 us -> 0 us
    unnamed x3 -> x0, local copies, waits for them, and re-layouts: 4.68 us -> none
    pallas_call x1, Pallas kernels: 41.1 us -> 39.7 us  [on_device(): pl.pallas_call(functools.partial(kernel, ndp, nseq, rollouts, sizes, stre...]
    pallas_call x0 -> x1, Pallas kernels: none -> 1 us  [on_device(): pl.pallas_call(finish, out_shape=(jax.ShapeDtypeStruct((1, tokens), f32),...]
where the time goes in v2:
time: 41.5 us; the launch traced here: 41.3 us
  Pallas kernels  40.7 us (98%)
  between operations  0.64 us (2%)
    pallas_call x1, Pallas kernels, on_device(): pl.pallas_call(functools.partial(kernel, ndp, nseq, rollouts, sizes, stre...  39.7 us
    pallas_call x1, Pallas kernels, on_device(): pl.pallas_call(finish, out_shape=(jax.ShapeDtypeStruct((1, tokens), f32),...  1 us

profile of v2, /device:TPU:0, one launch (start us, length us, event | category | flops | bytes accessed | tf_op | source)
XLA Modules:
  0.0 41.3 jit_solution(7783550507139984230)
XLA Ops:
  0.6 39.7 %shard_map.85 = (f32[1,1024]{1,0:T(1,128)S(1)}, f32[64,4096]{1,0:T(8,128)S(1)}, f32[1,64]{1,0:T(1,128)S(1)}) custom-call(bf16[1024,4096]{1,0:T(8,128)(2,1)} %bitcast.5, bf16[64,4096]{1,0:T(8,128)(2,1)} %bitcast.6, f32[1,64]{1,0:T(1,128)} %bitcast.7, f32[1,1024]{1,0:T(1,128)} %far_returns.1, s32[1,1024]{1,0:T(1,128)} %far_bins.1, s32[1,1024]{1,0:T(1,128)} %far_mask.1), custom_call_target="tpu_custom_call" | custom-call | tf_op jit(solution)/shard_map/pallas_call | solution.py:311
  40.3 1.0 %shard_map.86 = (f32[1,1024]{1,0:T(1,128)}, f32[64,4096]{1,0:T(8,128)}, f32[1,64]{1,0:T(1,128)}) custom-call(f32[1,1024]{1,0:T(1,128)S(1)} %get-tuple-element.9.targets, f32[64,4096]{1,0:T(8,128)S(1)} %get-tuple-element.10.grad, f32[1,64]{1,0:T(1,128)S(1)} %get-tuple-element.11.bias_grad), custom_call_target="tpu_custom_call" | custom-call | tf_op jit(solution)/shard_map/pallas_call | solution.py:345
